TPU v7x, 32 devices: a whole 2x2x4 slice. The times are simulated.
32 devices in a mesh: tm: 4 (over z), mem: 4 (over y, x), tile: 2 (over core).
Axes of the slice: x: 2, y: 2, z: 4, core: 2. Of those that a mesh axis runs over, the one named last changes fastest.
Arguments:
- control: float32 [40, 2, 8, 256], P('mem', None, 'tile'), may hold values from -6 to 6
- vertical_modes: float32 [64, 2], replicated, may hold values from -4 to 4
- mode_counts: int32 [8], P('tile'), may hold values from 1 to 2, as said below
- perturbations: bfloat16 [40, 8, 64, 8, 256], P('mem', 'tm', None, 'tile'), may hold values from -6 to 6
- slot_index: int32 [12], P('tm'), may hold values from 0 to 7, as said below
- blend_weight: float32 [12], P('tm'), may hold values from 0 to 1
Outputs:
- increment: float32 [12, 64, 8, 256], P('tm', None, 'tile')
Inputs may be any that keep to these rules, and one draw needn't show every extreme that they name: slot_index[w] // 2 == w // 3. `mode_counts`: both ends of the range occur.
All inputs are finite; a program needn't handle non-finite values.
Results may differ from a plain program's by a relative error of at most 0.0003.
Values sent between devices are 32-bit elements; how exact they have to be, the bound alone decides.
No kernel may reach another device: no remote copies, remote signals or barrier semaphores. Data moves between devices by JAX's collectives and lax.ppermute only.
A program may use at most 64 MiB of HBM per device.

v0:
```python
import math
import jax
import jax.numpy as jnp
from jax import lax
from jax.sharding import PartitionSpec as P

VM = 2
SMOOTH = 4
diffusion = 0.24


def ring(count, shift):
    return [(i, (i + shift) % count) for i in range(count)]


def is_power(count):
    return count & count - 1 == 0


def pairing(count, step):
    if is_power(count):
        return [(i, i ^ step) for i in range(count)]
    return ring(count, step)


def target_of(place, count, step):
    if is_power(count):
        return place ^ step
    return (place + step) % count


def source_of(place, count, step):
    if is_power(count):
        return place ^ step
    return (place - step) % count


def relax(field):
    neighbours = jnp.roll(field, -1, axis=2) + jnp.roll(field, 1, axis=2)
    bordered = jnp.pad(field, ((0, 0), (0, 0), (0, 0), (1, 1)))
    lateral = bordered[:, :, :, 2:] + bordered[:, :, :, :-2]
    return field + diffusion * (neighbours + lateral - 4.0 * field)


def smooth(field):
    count = lax.axis_size("tile")
    width = field.shape[2]
    left = SMOOTH
    while left:
        reach = min(left, width)
        if count == 1:
            wide, start = (field, 0)
        elif count == 2 and reach == width:
            other = lax.ppermute(field, "tile", ring(2, 1))
            wide, start = (jnp.concatenate([field, other], axis=2), 0)
        else:
            head = lax.slice_in_dim(field, 0, reach, axis=2)
            tail = lax.slice_in_dim(field, width - reach, width, axis=2)
            before = lax.ppermute(tail, "tile", ring(count, 1))
            after = lax.ppermute(head, "tile", ring(count, -1))
            wide, start = (jnp.concatenate([before, field, after], axis=2), reach)
        for _ in range(reach):
            wide = relax(wide)
        field = lax.slice_in_dim(wide, start, start + width, axis=2)
        left -= reach
    return field


def per_device(control, vertical_modes, mode_counts, perturbations, slot_index, blend_weight):
    members, slot_count, levels = perturbations.shape[:3]
    group = lax.axis_size("mem")
    place = lax.axis_index("mem")
    share = levels // group
    norm_factor = 1.0 / math.sqrt(members * group - 1)
    field = smooth(control)
    masked = []
    for mode_index in range(VM):
        keep_mode = (mode_index < mode_counts).astype(jnp.float32)
        masked.append(keep_mode[None, :, None] * field[:, mode_index])

    def terms(owner):
        part = lax.dynamic_slice_in_dim(perturbations, owner * share, share, axis=2)
        modes = lax.dynamic_slice_in_dim(vertical_modes, owner * share, share, axis=0)
        localized = sum((modes[:, m][None, :, None, None] * masked[m][:, None] for m in range(VM)))
        return jnp.sum(localized[:, None] * part.astype(jnp.float32), axis=0)

    arrived = []
    for step in range(group - 1, 0, -1):
        arrived.append(
            lax.ppermute(terms(target_of(place, group, step)), "mem", pairing(group, step))
        )
    slots = terms(place)
    for part in arrived:
        slots = slots + part
    slots = slots * norm_factor
    stages = lax.axis_size("tm")
    stage = lax.axis_index("tm")
    total = jnp.sum(slots, axis=0)
    earlier = jnp.zeros_like(total)
    for step in range(1, stages):
        came = lax.ppermute(total, "tm", ring(stages, step))
        earlier = earlier + jnp.where(stage >= step, came, 0.0)
    local_slot = slot_index - stage * slot_count
    blended = []
    for w in range(slot_index.shape[0]):
        mixed = earlier
        for s in range(slot_count):
            factor = jnp.where(
                local_slot[w] == s, blend_weight[w], jnp.where(local_slot[w] > s, 1.0, 0.0)
            )
            mixed = mixed + factor * slots[s]
        blended.append(mixed)
    blended = jnp.stack(blended)
    return lax.all_gather(blended, "mem", axis=1, tiled=True)


def solution(mesh):
    placed = (
        P("mem", None, "tile", None),
        P(),
        P("tile"),
        P("mem", "tm", None, "tile", None),
        P("tm"),
        P("tm"),
    )
    return jax.shard_map(
        per_device,
        mesh=mesh,
        in_specs=placed,
        out_specs=P("tm", None, "tile", None),
        check_vma=False,
    )
```

profile of v0, /device:TPU:0, one launch (start us, length us, event | category | flops | bytes accessed | tf_op | source)
XLA Modules:
  0.0 44.2 jit_solution(4025381710863709894)
XLA Ops:
  0.0 0.5 %collective-permute-start = (f32[10,2,4,256]{3,2,1,0:T(4,128)}, f32[10,2,4,256]{3,2,1,0:T(4,128)S(1)}, u32[]{:S(2)}, u32[]{:S(2)}) collective-permute-start(f32[10,2,4,256]{3,2,1,0:T(4,128)} %param.6), channel_id=1, source_target_pairs={{0,1},{1,0},{2,3},{3,2},{4,5},{5,4},{6,7},{7,6},{8,9},{9,8},{10,11... | collective-permute-start | bytes 245768 | tf_op jit(solution)/shard_map/ppermute | solution.py:54
  0.5 0.9 %constant_dynamic-slice_fusion.1 = (f32[16,2]{0,1:T(2,128)S(1)}, f32[16,2]{0,1:T(2,128)S(1)}, f32[16,2]{0,1:T(2,128)S(1)}, f32[16,2]{0,1:T(2,128)S(1)}) fusion(f32[64,2]{0,1:T(2,128)} %param.7, s32[]{:T(128)S(6)} %select_n.101, s32[]{:T(128)S(6)} %select_n.100, s32[]{:T(128)S(6)} %select_n.99, s32[]{:T(128)S(6)} %select_n.102), kind=kLoop, calls=%fused_computation.64 | loop fusion | bytes 1040 | tf_op jit(solution)/shard_map/dynamic_slice | solution.py:83
  1.4 0.7 %compare_convert_fusion.1 = (f32[4]{0:T(128)S(1)}, f32[4]{0:T(128)S(1)}) fusion(s32[4]{0:T(128)} %param.8), kind=kLoop, calls=%fused_computation.68 | loop fusion | flops 16 | bytes 48 | tf_op jit(solution)/shard_map/convert_element_type | solution.py:78
  2.1 0.9 %slice.153 = f32[10,2,1,256]{3,2,1,0:T(1,128)S(1)} slice(f32[10,2,4,256]{3,2,1,0:T(4,128)} %param.6), slice={[0:10], [0:2], [0:1], [0:256]} | slice | bytes 40960 | tf_op jit(solution)/shard_map/jit(_roll_static)/slice | solution.py:39
  3.0 0.0 collective-permute-done
  3.0 1.0 %fusion.1 = (f32[10,2,7,256]{3,2,1,0:T(8,128)S(1)}, f32[10,2,7,256]{3,2,1,0:T(8,128)S(1)}) fusion(f32[10,2,4,256]{3,2,1,0:T(4,128)} %param.6, f32[10,2,4,256]{3,2,1,0:T(4,128)S(1)} %collective-permute-done), kind=kLoop, calls=%fused_computation.23 | loop fusion | flops 71680 | bytes 450560 | tf_op jit(solution)/shard_map/concatenate | solution.py:55
  4.0 0.9 %pad_maximum_fusion = f32[10,2,8,256]{3,2,1,0:T(8,128)S(1)} fusion(f32[10,2,4,256]{3,2,1,0:T(4,128)S(1)} %collective-permute-done, f32[10,2,4,256]{3,2,1,0:T(4,128)} %param.6), kind=kLoop, calls=%fused_computation.18 | loop fusion | flops 40960 | bytes 327680 | tf_op jit(solution)/shard_map/concatenate | solution.py:55
  5.0 0.2 fusion.6
  5.2 0.2 fusion.11
  5.5 0.2 fusion.16
  5.7 0.2 fusion.21
  5.9 0.1 fusion.26
  5.9 0.0 copy-start
  6.0 0.8 %multiply_add_fusion.1 = (f32[10,16,4,256]{3,2,1,0:T(4,128)S(1)}, f32[10,16,4,256]{3,2,1,0:T(4,128)S(1)}, f32[10,16,4,256]{3,2,1,0:T(4,128)S(1)}, f32[10,16,4,256]{3,2,1,0:T(4,128)S(1)}) fusion(f32[16]{0:T(128)S(1)} %get-tuple-element.55, f32[16]{0:T(128)S(1)} %get-tuple-element.56, f32[10,4,256]{2,1,0:T(4,128)S(1)} %get-tuple-element.16, ...), kind=kLoop, calls=%fused_computation.5 | loop fusion | flops 1966080 | bytes 2703872 | tf_op jit(solution)/shard_map/add | solution.py:84
  6.7 1.0 %copy-done = bf16[10,2,64,4,256]{4,3,2,1,0:T(4,128)(2,1)S(1)} copy-done((bf16[10,2,64,4,256]{4,3,2,1,0:T(4,128)(2,1)S(1)}, bf16[10,2,64,4,256]{4,3,2,1,0:T(4,128)(2,1)}, u32[]{:S(2)}) %copy-start) | copy-done | bytes 2621464
  7.7 0.0 copy-start.2
  7.7 0.0 copy-start.1
  7.7 1.5 %multiply_reduce_fusion.2 = (f32[2,16,4,256]{3,2,1,0:T(4,128)S(1)}, f32[2,16,4,256]{3,2,1,0:T(4,128)S(1)}, f32[2,16,4,256]{3,2,1,0:T(4,128)S(1)}, f32[2,16,4,256]{3,2,1,0:T(4,128)S(1)}) fusion(bf16[10,2,64,4,256]{4,3,2,1,0:T(4,128)(2,1)S(1)} %copy-done, s32[]{:T(128)S(6)} %select_n.100, f32[10,16,4,256]{3,2,1,0:T(4,128)S(1)} %get-tuple-element.32, ...), kind=kLoop, calls=%fused_computation.2 | loop fusion | flops 3801088 | bytes 5767184 | tf_op jit(solution)/shard_map/reduce_sum | solution.py:85
  9.2 3.5 %collective-permute-start.1 = (f32[2,16,4,256]{3,2,1,0:T(4,128)S(1)}, f32[2,16,4,256]{3,2,1,0:T(4,128)S(1)}, u32[]{:S(2)}, u32[]{:S(2)}) collective-permute-start(f32[2,16,4,256]{3,2,1,0:T(4,128)S(1)} %get-tuple-element.5), channel_id=1, source_target_pairs={{0,6},{2,4},{4,2},{6,0},{1,7},{3,5},{5,3},{7,1},{8,14},{10,12},{12... | collective-permute-start | bytes 393224 | tf_op jit(solution)/shard_map/ppermute | solution.py:90
  12.7 0.5 %collective-permute-start.2 = (f32[2,16,4,256]{3,2,1,0:T(4,128)S(1)}, f32[2,16,4,256]{3,2,1,0:T(4,128)S(1)}, u32[]{:S(2)}, u32[]{:S(2)}) collective-permute-start(f32[2,16,4,256]{3,2,1,0:T(4,128)S(1)} %get-tuple-element.8), channel_id=1, source_target_pairs={{0,4},{2,6},{4,0},{6,2},{1,5},{3,7},{5,1},{7,3},{8,12},{10,14},{12... | collective-permute-start | bytes 393224 | tf_op jit(solution)/shard_map/ppermute | solution.py:90
  13.2 0.1 collective-permute-start.3
  13.4 0.0 copy-done.2
  13.4 0.7 %fusion.35 = (s32[1]{0:T(128)}, s32[1]{0:T(128)}, s32[1]{0:T(128)}) fusion(s32[3]{0:T(128)S(1)} %broadcast_subtract_fusion), kind=kLoop, calls=%fused_computation.86 | loop fusion | bytes 24 | tf_op jit(solution)/shard_map/slice | solution.py:109
  21.7 0.0 collective-permute-done.1
  21.7 0.0 collective-permute-done.2
  21.7 0.0 collective-permute-done.3
  21.7 0.1 fusion.27
  21.8 2.0 %collective-permute-start.4 = (f32[16,4,256]{2,1,0:T(4,128)S(1)}, f32[16,4,256]{2,1,0:T(4,128)S(1)}, u32[]{:S(2)}, u32[]{:S(2)}) collective-permute-start(f32[16,4,256]{2,1,0:T(4,128)S(1)} %get-tuple-element.11), channel_id=1, source_target_pairs={{0,8},{8,16},{16,24},{24,0},{1,9},{9,17},{17,25},{25,1},{2,10},{10... | collective-permute-start | bytes 196616 | tf_op jit(solution)/shard_map/ppermute | solution.py:101
  23.8 2.6 %collective-permute-start.5 = (f32[16,4,256]{2,1,0:T(4,128)S(1)}, f32[16,4,256]{2,1,0:T(4,128)S(1)}, u32[]{:S(2)}, u32[]{:S(2)}) collective-permute-start(f32[16,4,256]{2,1,0:T(4,128)S(1)} %get-tuple-element.11), channel_id=1, source_target_pairs={{0,16},{8,24},{16,0},{24,8},{1,17},{9,25},{17,1},{25,9},{2,18},{10... | collective-permute-start | bytes 196616 | tf_op jit(solution)/shard_map/ppermute | solution.py:101
  26.4 1.3 %collective-permute-start.6 = (f32[16,4,256]{2,1,0:T(4,128)S(1)}, f32[16,4,256]{2,1,0:T(4,128)S(1)}, u32[]{:S(2)}, u32[]{:S(2)}) collective-permute-start(f32[16,4,256]{2,1,0:T(4,128)S(1)} %get-tuple-element.11), channel_id=1, source_target_pairs={{0,24},{8,0},{16,8},{24,16},{1,25},{9,1},{17,9},{25,17},{2,26},{10... | collective-permute-start | bytes 196616 | tf_op jit(solution)/shard_map/ppermute | solution.py:101
  27.8 0.0 copy-done.1
  27.8 0.6 %fusion.34 = (f32[1]{0:T(128)}, f32[1]{0:T(128)}, f32[1]{0:T(128)}) fusion(f32[3]{0:T(128)S(1)} %copy-done.1), kind=kLoop, calls=%fused_computation.85 | loop fusion | bytes 24 | tf_op jit(solution)/shard_map/slice | solution.py:109
  32.0 0.0 collective-permute-done.4
  32.0 0.0 collective-permute-done.5
  32.0 0.0 collective-permute-done.6
  32.1 0.1 fusion.24
  32.2 11.1 %all_gather.3 = f32[3,64,4,256]{3,2,1,0:T(4,128)S(1)} all-gather(f32[3,16,4,256]{3,2,1,0:T(4,128)S(1)} %pad_maximum_fusion.1), channel_id=1, replica_groups=mesh['tm'=4,'mem'=4,'tile'=2] {'mem'}, dimensions={1}, use_global_device_ids=true | all-gather | bytes 983040 | tf_op jit(solution)/shard_map/all_gather | solution.py:114
  43.4 0.9 %copy.8 = f32[3,64,4,256]{3,2,1,0:T(4,128)} copy(f32[3,64,4,256]{3,2,1,0:T(4,128)S(1)} %all_gather.3) | data formatting | bytes 1572864
  (12 shorter events, 0.3 us)
Async XLA Ops:
  0.0 3.0 %collective-permute-start = (f32[10,2,4,256]{3,2,1,0:T(4,128)}, f32[10,2,4,256]{3,2,1,0:T(4,128)S(1)}, u32[]{:S(2)}, u32[]{:S(2)}) collective-permute-start(f32[10,2,4,256]{3,2,1,0:T(4,128)} %param.6), channel_id=1, source_target_pairs={{0,1},{1,0},{2,3},{3,2},{4,5},{5,4},{6,7},{7,6},{8,9},{9,8},{10,11... | collective-permute-start | bytes 245768 | tf_op jit(solution)/shard_map/ppermute | solution.py:54
  5.9 1.7 %copy-start = (bf16[10,2,64,4,256]{4,3,2,1,0:T(4,128)(2,1)S(1)}, bf16[10,2,64,4,256]{4,3,2,1,0:T(4,128)(2,1)}, u32[]{:S(2)}) copy-start(bf16[10,2,64,4,256]{4,3,2,1,0:T(4,128)(2,1)} %param.9) | copy-start | bytes 7864324
  7.7 5.7 %copy-start.2 = (s32[3]{0:T(128)S(1)}, s32[3]{0:T(128)}, u32[]{:S(2)}) copy-start(s32[3]{0:T(128)} %param.10) | copy-start | bytes 40
  7.7 20.1 %copy-start.1 = (f32[3]{0:T(128)S(1)}, f32[3]{0:T(128)}, u32[]{:S(2)}) copy-start(f32[3]{0:T(128)} %param.11) | copy-start | bytes 40
  9.2 12.4 %collective-permute-start.1 = (f32[2,16,4,256]{3,2,1,0:T(4,128)S(1)}, f32[2,16,4,256]{3,2,1,0:T(4,128)S(1)}, u32[]{:S(2)}, u32[]{:S(2)}) collective-permute-start(f32[2,16,4,256]{3,2,1,0:T(4,128)S(1)} %get-tuple-element.5), channel_id=1, source_target_pairs={{0,6},{2,4},{4,2},{6,0},{1,7},{3,5},{5,3},{7,1},{8,14},{10,12},{12... | collective-permute-start | bytes 393224 | tf_op jit(solution)/shard_map/ppermute | solution.py:90
  12.7 8.9 %collective-permute-start.2 = (f32[2,16,4,256]{3,2,1,0:T(4,128)S(1)}, f32[2,16,4,256]{3,2,1,0:T(4,128)S(1)}, u32[]{:S(2)}, u32[]{:S(2)}) collective-permute-start(f32[2,16,4,256]{3,2,1,0:T(4,128)S(1)} %get-tuple-element.8), channel_id=1, source_target_pairs={{0,4},{2,6},{4,0},{6,2},{1,5},{3,7},{5,1},{7,3},{8,12},{10,14},{12... | collective-permute-start | bytes 393224 | tf_op jit(solution)/shard_map/ppermute | solution.py:90
  13.2 8.4 %collective-permute-start.3 = (f32[2,16,4,256]{3,2,1,0:T(4,128)S(1)}, f32[2,16,4,256]{3,2,1,0:T(4,128)S(1)}, u32[]{:S(2)}, u32[]{:S(2)}) collective-permute-start(f32[2,16,4,256]{3,2,1,0:T(4,128)S(1)} %get-tuple-element.7), channel_id=1, source_target_pairs={{0,2},{2,0},{4,6},{6,4},{1,3},{3,1},{5,7},{7,5},{8,10},{10,8},{12,... | collective-permute-start | bytes 393224 | tf_op jit(solution)/shard_map/ppermute | solution.py:90
  21.8 10.2 %collective-permute-start.4 = (f32[16,4,256]{2,1,0:T(4,128)S(1)}, f32[16,4,256]{2,1,0:T(4,128)S(1)}, u32[]{:S(2)}, u32[]{:S(2)}) collective-permute-start(f32[16,4,256]{2,1,0:T(4,128)S(1)} %get-tuple-element.11), channel_id=1, source_target_pairs={{0,8},{8,16},{16,24},{24,0},{1,9},{9,17},{17,25},{25,1},{2,10},{10... | collective-permute-start | bytes 196616 | tf_op jit(solution)/shard_map/ppermute | solution.py:101
  23.8 8.2 %collective-permute-start.5 = (f32[16,4,256]{2,1,0:T(4,128)S(1)}, f32[16,4,256]{2,1,0:T(4,128)S(1)}, u32[]{:S(2)}, u32[]{:S(2)}) collective-permute-start(f32[16,4,256]{2,1,0:T(4,128)S(1)} %get-tuple-element.11), channel_id=1, source_target_pairs={{0,16},{8,24},{16,0},{24,8},{1,17},{9,25},{17,1},{25,9},{2,18},{10... | collective-permute-start | bytes 196616 | tf_op jit(solution)/shard_map/ppermute | solution.py:101
  26.4 5.6 %collective-permute-start.6 = (f32[16,4,256]{2,1,0:T(4,128)S(1)}, f32[16,4,256]{2,1,0:T(4,128)S(1)}, u32[]{:S(2)}, u32[]{:S(2)}) collective-permute-start(f32[16,4,256]{2,1,0:T(4,128)S(1)} %get-tuple-element.11), channel_id=1, source_target_pairs={{0,24},{8,0},{16,8},{24,16},{1,25},{9,1},{17,9},{25,17},{2,26},{10... | collective-permute-start | bytes 196616 | tf_op jit(solution)/shard_map/ppermute | solution.py:101
where the time goes:
time: 44.7 us; the launch traced here: 44.2 us
  between operations  11.5 us (26%)
  blocking collectives  11.1 us (25%)
  starting transfers between devices  10.6 us (24%)
  other arithmetic  5.92 us (13%)
  local copies, waits for them, and re-layouts  5.11 us (11%)
    all_gather x1, blocking collectives, per_device(): return lax.all_gather(blended, 'mem', axis=1, tiled=True)  11.1 us
    ppermute x3, starting transfers between devices, per_device(): came = lax.ppermute(total, 'tm', ring(stages, step))  5.97 us
    ppermute x3, starting transfers between devices, per_device(): lax.ppermute(terms(target_of(place, group, step)), 'mem', pairing(group,...  4.14 us
    concatenate x2, other arithmetic, smooth(): wide, start = (jnp.concatenate([field, other], axis=2), 0)  1.96 us
    unnamed x7, local copies, waits for them, and re-layouts  1.85 us
    reduce_sum x1, other arithmetic, terms(): return jnp.sum(localized[:, None] * part.astype(jnp.float32), axis=0)  1.54 us
    slice x8, local copies, waits for them, and re-layouts, relax(): neighbours = jnp.roll(field, -1, axis=2) + jnp.roll(field, 1, axis=2)  1.08 us
    dynamic_slice x1, local copies, waits for them, and re-layouts, terms(): lax.dynamic_slice_in_dim(vertical_modes, owner * share, share, axis=0)  0.9 us
  transfers between devices with their start and end apart: 7, of which 0 were waited for; matrix products, arithmetic and copies ran while one was open for 8% of the time, Pallas kernels for 0%

commit v1 on v0

--- a/solution.py
+++ b/solution.py
@@ -111,7 +111,9 @@
             mixed = mixed + factor * slots[s]
         blended.append(mixed)
     blended = jnp.stack(blended)
-    return lax.all_gather(blended, "mem", axis=1, tiled=True)
+    return jnp.concatenate(
+        lax.all_to_all(jnp.stack([blended] * lax.axis_size("mem")), "mem", 0, 0), axis=1
+    )
 
 
 def solution(mesh):

time: 44.7 us -> 48.2 us (1.078)
  blocking collectives: 11.1 us -> 13.8 us
  local copies, waits for them, and re-layouts: 5.11 us -> 5.89 us
    all_to_all x0 -> x1, blocking collectives: none -> 13.8 us  [per_device(): lax.all_to_all(jnp.stack([blended] * lax.axis_size('mem')), 'mem', 0, 0)]
    all_gather x1 -> x0, blocking collectives: 11.1 us -> none  [per_device(): return lax.all_gather(blended, 'mem', axis=1, tiled=True)]
    reshape x0 -> x1, local copies, waits for them, and re-layouts: none -> 1.39 us  [per_device(): jnp.concatenate(lax.all_to_all(jnp.stack([blended] * lax.axis_size('mem')...]
    unnamed x7 -> x6, local copies, waits for them, and re-layouts: 1.85 us -> 0.97 us
where the time goes in v1:
time: 48.2 us; the launch traced here: 47.7 us
  blocking collectives  13.8 us (29%)
  between operations  11.5 us (24%)
  starting transfers between devices  10.6 us (22%)
  other arithmetic  5.92 us (12%)
  local copies, waits for them, and re-layouts  5.89 us (12%)
    all_to_all x1, blocking collectives, per_device(): lax.all_to_all(jnp.stack([blended] * lax.axis_size('mem')), 'mem', 0, 0)  13.8 us
    ppermute x3, starting transfers between devices, per_device(): came = lax.ppermute(total, 'tm', ring(stages, step))  5.97 us
    ppermute x3, starting transfers between devices, per_device(): lax.ppermute(terms(target_of(place, group, step)), 'mem', pairing(group,...  4.14 us
    concatenate x2, other arithmetic, smooth(): wide, start = (jnp.concatenate([field, other], axis=2), 0)  1.96 us
    reduce_sum x1, other arithmetic, terms(): return jnp.sum(localized[:, None] * part.astype(jnp.float32), axis=0)  1.54 us
    reshape x1, local copies, waits for them, and re-layouts, per_device(): jnp.concatenate(lax.all_to_all(jnp.stack([blended] * lax.axis_size('mem')...  1.39 us
    slice x8, local copies, waits for them, and re-layouts, relax(): neighbours = jnp.roll(field, -1, axis=2) + jnp.roll(field, 1, axis=2)  1.08 us
    unnamed x6, local copies, waits for them, and re-layouts  0.97 us
  transfers between devices with their start and end apart: 7, of which 0 were waited for; matrix products, arithmetic and copies ran while one was open for 8% of the time, Pallas kernels for 0%

profile of v1, /device:TPU:0, one launch (start us, length us, event | category | flops | bytes accessed | tf_op | source)
XLA Modules:
  0.0 47.7 jit_solution(12814436466504905702)
XLA Ops:
  0.0 0.5 %collective-permute-start = (f32[10,2,4,256]{3,2,1,0:T(4,128)}, f32[10,2,4,256]{3,2,1,0:T(4,128)S(1)}, u32[]{:S(2)}, u32[]{:S(2)}) collective-permute-start(f32[10,2,4,256]{3,2,1,0:T(4,128)} %param.6), channel_id=1, source_target_pairs={{0,1},{1,0},{2,3},{3,2},{4,5},{5,4},{6,7},{7,6},{8,9},{9,8},{10,11... | collective-permute-start | bytes 245768 | tf_op jit(solution)/shard_map/ppermute | solution.py:54
  0.5 0.9 %constant_dynamic-slice_fusion.1 = (f32[16,2]{0,1:T(2,128)S(1)}, f32[16,2]{0,1:T(2,128)S(1)}, f32[16,2]{0,1:T(2,128)S(1)}, f32[16,2]{0,1:T(2,128)S(1)}) fusion(f32[64,2]{0,1:T(2,128)} %param.7, s32[]{:T(128)S(6)} %select_n.101, s32[]{:T(128)S(6)} %select_n.100, s32[]{:T(128)S(6)} %select_n.99, s32[]{:T(128)S(6)} %select_n.102), kind=kLoop, calls=%fused_computation.64 | loop fusion | bytes 1040 | tf_op jit(solution)/shard_map/dynamic_slice | solution.py:83
  1.4 0.7 %compare_convert_fusion.1 = (f32[4]{0:T(128)S(1)}, f32[4]{0:T(128)S(1)}) fusion(s32[4]{0:T(128)} %param.8), kind=kLoop, calls=%fused_computation.68 | loop fusion | flops 16 | bytes 48 | tf_op jit(solution)/shard_map/convert_element_type | solution.py:78
  2.1 0.9 %slice.153 = f32[10,2,1,256]{3,2,1,0:T(1,128)S(1)} slice(f32[10,2,4,256]{3,2,1,0:T(4,128)} %param.6), slice={[0:10], [0:2], [0:1], [0:256]} | slice | bytes 40960 | tf_op jit(solution)/shard_map/jit(_roll_static)/slice | solution.py:39
  3.0 0.0 collective-permute-done
  3.0 1.0 %fusion.1 = (f32[10,2,7,256]{3,2,1,0:T(8,128)S(1)}, f32[10,2,7,256]{3,2,1,0:T(8,128)S(1)}) fusion(f32[10,2,4,256]{3,2,1,0:T(4,128)} %param.6, f32[10,2,4,256]{3,2,1,0:T(4,128)S(1)} %collective-permute-done), kind=kLoop, calls=%fused_computation.23 | loop fusion | flops 71680 | bytes 450560 | tf_op jit(solution)/shard_map/concatenate | solution.py:55
  4.0 0.9 %pad_maximum_fusion = f32[10,2,8,256]{3,2,1,0:T(8,128)S(1)} fusion(f32[10,2,4,256]{3,2,1,0:T(4,128)S(1)} %collective-permute-done, f32[10,2,4,256]{3,2,1,0:T(4,128)} %param.6), kind=kLoop, calls=%fused_computation.18 | loop fusion | flops 40960 | bytes 327680 | tf_op jit(solution)/shard_map/concatenate | solution.py:55
  5.0 0.2 fusion.6
  5.2 0.2 fusion.11
  5.5 0.2 fusion.16
  5.7 0.2 fusion.21
  5.9 0.1 fusion.26
  5.9 0.0 copy-start
  6.0 0.8 %multiply_add_fusion.1 = (f32[10,16,4,256]{3,2,1,0:T(4,128)S(1)}, f32[10,16,4,256]{3,2,1,0:T(4,128)S(1)}, f32[10,16,4,256]{3,2,1,0:T(4,128)S(1)}, f32[10,16,4,256]{3,2,1,0:T(4,128)S(1)}) fusion(f32[16]{0:T(128)S(1)} %get-tuple-element.55, f32[16]{0:T(128)S(1)} %get-tuple-element.56, f32[10,4,256]{2,1,0:T(4,128)S(1)} %get-tuple-element.16, ...), kind=kLoop, calls=%fused_computation.5 | loop fusion | flops 1966080 | bytes 2703872 | tf_op jit(solution)/shard_map/add | solution.py:84
  6.7 1.0 %copy-done = bf16[10,2,64,4,256]{4,3,2,1,0:T(4,128)(2,1)S(1)} copy-done((bf16[10,2,64,4,256]{4,3,2,1,0:T(4,128)(2,1)S(1)}, bf16[10,2,64,4,256]{4,3,2,1,0:T(4,128)(2,1)}, u32[]{:S(2)}) %copy-start) | copy-done | bytes 2621464
  7.7 0.0 copy-start.2
  7.7 0.0 copy-start.1
  7.7 1.5 %multiply_reduce_fusion.2 = (f32[2,16,4,256]{3,2,1,0:T(4,128)S(1)}, f32[2,16,4,256]{3,2,1,0:T(4,128)S(1)}, f32[2,16,4,256]{3,2,1,0:T(4,128)S(1)}, f32[2,16,4,256]{3,2,1,0:T(4,128)S(1)}) fusion(bf16[10,2,64,4,256]{4,3,2,1,0:T(4,128)(2,1)S(1)} %copy-done, s32[]{:T(128)S(6)} %select_n.100, f32[10,16,4,256]{3,2,1,0:T(4,128)S(1)} %get-tuple-element.32, ...), kind=kLoop, calls=%fused_computation.2 | loop fusion | flops 3801088 | bytes 5767184 | tf_op jit(solution)/shard_map/reduce_sum | solution.py:85
  9.2 3.5 %collective-permute-start.1 = (f32[2,16,4,256]{3,2,1,0:T(4,128)S(1)}, f32[2,16,4,256]{3,2,1,0:T(4,128)S(1)}, u32[]{:S(2)}, u32[]{:S(2)}) collective-permute-start(f32[2,16,4,256]{3,2,1,0:T(4,128)S(1)} %get-tuple-element.5), channel_id=1, source_target_pairs={{0,6},{2,4},{4,2},{6,0},{1,7},{3,5},{5,3},{7,1},{8,14},{10,12},{12... | collective-permute-start | bytes 393224 | tf_op jit(solution)/shard_map/ppermute | solution.py:90
  12.7 0.5 %collective-permute-start.2 = (f32[2,16,4,256]{3,2,1,0:T(4,128)S(1)}, f32[2,16,4,256]{3,2,1,0:T(4,128)S(1)}, u32[]{:S(2)}, u32[]{:S(2)}) collective-permute-start(f32[2,16,4,256]{3,2,1,0:T(4,128)S(1)} %get-tuple-element.8), channel_id=1, source_target_pairs={{0,4},{2,6},{4,0},{6,2},{1,5},{3,7},{5,1},{7,3},{8,12},{10,14},{12... | collective-permute-start | bytes 393224 | tf_op jit(solution)/shard_map/ppermute | solution.py:90
  13.2 0.1 collective-permute-start.3
  13.4 0.0 copy-done.2
  13.4 0.7 %fusion.35 = (s32[1]{0:T(128)}, s32[1]{0:T(128)}, s32[1]{0:T(128)}) fusion(s32[3]{0:T(128)S(1)} %broadcast_subtract_fusion), kind=kLoop, calls=%fused_computation.86 | loop fusion | bytes 24 | tf_op jit(solution)/shard_map/slice | solution.py:109
  21.7 0.0 collective-permute-done.1
  21.7 0.0 collective-permute-done.2
  21.7 0.0 collective-permute-done.3
  21.7 0.1 fusion.27
  21.8 2.0 %collective-permute-start.4 = (f32[16,4,256]{2,1,0:T(4,128)S(1)}, f32[16,4,256]{2,1,0:T(4,128)S(1)}, u32[]{:S(2)}, u32[]{:S(2)}) collective-permute-start(f32[16,4,256]{2,1,0:T(4,128)S(1)} %get-tuple-element.11), channel_id=1, source_target_pairs={{0,8},{8,16},{16,24},{24,0},{1,9},{9,17},{17,25},{25,1},{2,10},{10... | collective-permute-start | bytes 196616 | tf_op jit(solution)/shard_map/ppermute | solution.py:101
  23.8 2.6 %collective-permute-start.5 = (f32[16,4,256]{2,1,0:T(4,128)S(1)}, f32[16,4,256]{2,1,0:T(4,128)S(1)}, u32[]{:S(2)}, u32[]{:S(2)}) collective-permute-start(f32[16,4,256]{2,1,0:T(4,128)S(1)} %get-tuple-element.11), channel_id=1, source_target_pairs={{0,16},{8,24},{16,0},{24,8},{1,17},{9,25},{17,1},{25,9},{2,18},{10... | collective-permute-start | bytes 196616 | tf_op jit(solution)/shard_map/ppermute | solution.py:101
  26.4 1.3 %collective-permute-start.6 = (f32[16,4,256]{2,1,0:T(4,128)S(1)}, f32[16,4,256]{2,1,0:T(4,128)S(1)}, u32[]{:S(2)}, u32[]{:S(2)}) collective-permute-start(f32[16,4,256]{2,1,0:T(4,128)S(1)} %get-tuple-element.11), channel_id=1, source_target_pairs={{0,24},{8,0},{16,8},{24,16},{1,25},{9,1},{17,9},{25,17},{2,26},{10... | collective-permute-start | bytes 196616 | tf_op jit(solution)/shard_map/ppermute | solution.py:101
  27.8 0.0 copy-done.1
  27.8 0.6 %fusion.34 = (f32[1]{0:T(128)}, f32[1]{0:T(128)}, f32[1]{0:T(128)}) fusion(f32[3]{0:T(128)S(1)} %copy-done.1), kind=kLoop, calls=%fused_computation.85 | loop fusion | bytes 24 | tf_op jit(solution)/shard_map/slice | solution.py:109
  32.0 0.0 collective-permute-done.4
  32.0 0.0 collective-permute-done.5
  32.0 0.0 collective-permute-done.6
  32.1 0.1 fusion.24
  32.2 0.1 stack.23
  32.4 13.8 %all_to_all.5 = f32[4,3,16,4,256]{4,3,2,1,0:T(4,128)S(1)} all-to-all(f32[4,3,16,4,256]{4,3,2,1,0:T(4,128)S(1)} %stack.23), channel_id=1, replica_groups=mesh['tm'=4,'mem'=4,'tile'=2] {'mem'}, dimensions={0} | all-to-all | bytes 1572864 | tf_op jit(solution)/shard_map/all_to_all | solution.py:115
  46.2 0.1 copy.7
  46.3 1.4 %copy.8 = f32[3,64,4,256]{3,2,1,0:T(4,128)} copy(f32[3,64,4,256]{3,1,2,0:T(8,128)S(1)} %bitcast.59) | data formatting | bytes 1572864 | tf_op jit(solution)/shard_map/reshape | solution.py:114
  (12 shorter events, 0.3 us)
Async XLA Ops:
  0.0 3.0 %collective-permute-start = (f32[10,2,4,256]{3,2,1,0:T(4,128)}, f32[10,2,4,256]{3,2,1,0:T(4,128)S(1)}, u32[]{:S(2)}, u32[]{:S(2)}) collective-permute-start(f32[10,2,4,256]{3,2,1,0:T(4,128)} %param.6), channel_id=1, source_target_pairs={{0,1},{1,0},{2,3},{3,2},{4,5},{5,4},{6,7},{7,6},{8,9},{9,8},{10,11... | collective-permute-start | bytes 245768 | tf_op jit(solution)/shard_map/ppermute | solution.py:54
  5.9 1.7 %copy-start = (bf16[10,2,64,4,256]{4,3,2,1,0:T(4,128)(2,1)S(1)}, bf16[10,2,64,4,256]{4,3,2,1,0:T(4,128)(2,1)}, u32[]{:S(2)}) copy-start(bf16[10,2,64,4,256]{4,3,2,1,0:T(4,128)(2,1)} %param.9) | copy-start | bytes 7864324
  7.7 5.7 %copy-start.2 = (s32[3]{0:T(128)S(1)}, s32[3]{0:T(128)}, u32[]{:S(2)}) copy-start(s32[3]{0:T(128)} %param.10) | copy-start | bytes 40
  7.7 20.1 %copy-start.1 = (f32[3]{0:T(128)S(1)}, f32[3]{0:T(128)}, u32[]{:S(2)}) copy-start(f32[3]{0:T(128)} %param.11) | copy-start | bytes 40
  9.2 12.4 %collective-permute-start.1 = (f32[2,16,4,256]{3,2,1,0:T(4,128)S(1)}, f32[2,16,4,256]{3,2,1,0:T(4,128)S(1)}, u32[]{:S(2)}, u32[]{:S(2)}) collective-permute-start(f32[2,16,4,256]{3,2,1,0:T(4,128)S(1)} %get-tuple-element.5), channel_id=1, source_target_pairs={{0,6},{2,4},{4,2},{6,0},{1,7},{3,5},{5,3},{7,1},{8,14},{10,12},{12... | collective-permute-start | bytes 393224 | tf_op jit(solution)/shard_map/ppermute | solution.py:90
  12.7 8.9 %collective-permute-start.2 = (f32[2,16,4,256]{3,2,1,0:T(4,128)S(1)}, f32[2,16,4,256]{3,2,1,0:T(4,128)S(1)}, u32[]{:S(2)}, u32[]{:S(2)}) collective-permute-start(f32[2,16,4,256]{3,2,1,0:T(4,128)S(1)} %get-tuple-element.8), channel_id=1, source_target_pairs={{0,4},{2,6},{4,0},{6,2},{1,5},{3,7},{5,1},{7,3},{8,12},{10,14},{12... | collective-permute-start | bytes 393224 | tf_op jit(solution)/shard_map/ppermute | solution.py:90
  13.2 8.4 %collective-permute-start.3 = (f32[2,16,4,256]{3,2,1,0:T(4,128)S(1)}, f32[2,16,4,256]{3,2,1,0:T(4,128)S(1)}, u32[]{:S(2)}, u32[]{:S(2)}) collective-permute-start(f32[2,16,4,256]{3,2,1,0:T(4,128)S(1)} %get-tuple-element.7), channel_id=1, source_target_pairs={{0,2},{2,0},{4,6},{6,4},{1,3},{3,1},{5,7},{7,5},{8,10},{10,8},{12,... | collective-permute-start | bytes 393224 | tf_op jit(solution)/shard_map/ppermute | solution.py:90
  21.8 10.2 %collective-permute-start.4 = (f32[16,4,256]{2,1,0:T(4,128)S(1)}, f32[16,4,256]{2,1,0:T(4,128)S(1)}, u32[]{:S(2)}, u32[]{:S(2)}) collective-permute-start(f32[16,4,256]{2,1,0:T(4,128)S(1)} %get-tuple-element.11), channel_id=1, source_target_pairs={{0,8},{8,16},{16,24},{24,0},{1,9},{9,17},{17,25},{25,1},{2,10},{10... | collective-permute-start | bytes 196616 | tf_op jit(solution)/shard_map/ppermute | solution.py:101
  23.8 8.2 %collective-permute-start.5 = (f32[16,4,256]{2,1,0:T(4,128)S(1)}, f32[16,4,256]{2,1,0:T(4,128)S(1)}, u32[]{:S(2)}, u32[]{:S(2)}) collective-permute-start(f32[16,4,256]{2,1,0:T(4,128)S(1)} %get-tuple-element.11), channel_id=1, source_target_pairs={{0,16},{8,24},{16,0},{24,8},{1,17},{9,25},{17,1},{25,9},{2,18},{10... | collective-permute-start | bytes 196616 | tf_op jit(solution)/shard_map/ppermute | solution.py:101
  26.4 5.6 %collective-permute-start.6 = (f32[16,4,256]{2,1,0:T(4,128)S(1)}, f32[16,4,256]{2,1,0:T(4,128)S(1)}, u32[]{:S(2)}, u32[]{:S(2)}) collective-permute-start(f32[16,4,256]{2,1,0:T(4,128)S(1)} %get-tuple-element.11), channel_id=1, source_target_pairs={{0,24},{8,0},{16,8},{24,16},{1,25},{9,1},{17,9},{25,17},{2,26},{10... | collective-permute-start | bytes 196616 | tf_op jit(solution)/shard_map/ppermute | solution.py:101
